TPU v7x, 256 devices: a whole 4x4x8 slice. The times are simulated.
256 devices in a mesh: arcs: 2 (over z_lo), trow: 8 (over y, core), tcol: 16 (over x, z_hi).
Axes of the slice: x: 4, y: 4, z: 8 (z_hi: 4, z_lo: 2; z = z_hi * 2 + z_lo), core: 2. Of those that a mesh axis runs over, the one named last changes fastest.
Arguments:
- design: bfloat16 [4096, 12288], P(('arcs', 'tcol'), 'trow'), may hold values from -6 to 6
- observed: float32 [4096], P(('arcs', 'tcol')), may hold values from -6 to 6
- arc_counts: int32 [128], P(('arcs', 'tcol')), may hold values from 2 to 32
- arc_weight: float32 [128], P(('arcs', 'tcol')), may hold values from 0.3 to 3
Outputs:
- gram: float32 [12288, 12288], P('trow', ('arcs', 'tcol'))
- rhs: float32 [12288], P('trow')
Inputs may be any that keep to these rules, and one draw needn't show every extreme that they name: `arc_counts`: each arc has at least two valid observations.
All inputs are finite; a program needn't handle non-finite values.
Results may differ from a plain program's by a relative error of at most 0.0055.
Values may be sent and summed in bfloat16 or wider, within the bound.
No kernel may reach another device: no remote copies, remote signals or barrier semaphores. Data moves between devices by JAX's collectives and lax.ppermute only.
A program may use at most 192 MiB of HBM per device.

v0:
```python
import jax
import jax.numpy as jnp
from jax import lax
from jax.sharding import PartitionSpec as P


def from_everyone(x, axis):
    devices = lax.axis_size(axis)
    return lax.all_to_all(jnp.broadcast_to(x[None], (devices, *x.shape)), axis, 0, 0, tiled=True)


def over_copies(x, axis):
    return from_everyone(x, axis).sum(axis=0)


def cut_along(x, dim, devices):
    dims = x.shape
    blocks = x.reshape(*dims[:dim], devices, dims[dim] // devices, *dims[dim + 1 :])
    return jnp.moveaxis(blocks, dim, 0)


def sum_at_owner(x, axis, dim):
    blocks = cut_along(x, dim, lax.axis_size(axis))
    arrived = lax.all_to_all(blocks, axis, split_axis=0, concat_axis=0, tiled=True)
    return arrived.astype(jnp.float32).sum(axis=0)


def fold_with(right, piece):
    return lax.dot_general(
        piece, right, (((0,), (0,)), ((), ())), preferred_element_type=jnp.float32
    )


def local(design, observed, arc_counts, arc_weight):
    row_count, col_width = design.shape
    arc_total = arc_counts.shape[0]
    arc_len = row_count // arc_total
    slot_index = lax.broadcasted_iota(jnp.int32, (arc_total, arc_len), 1)
    valid_mask = (slot_index < arc_counts[:, None]).astype(jnp.float32)
    counts_float = arc_counts.astype(jnp.float32)
    factor = valid_mask * jnp.sqrt(arc_weight)[:, None]
    blocks = design.reshape(arc_total, arc_len, col_width).astype(jnp.float32)
    column_mean = jnp.sum(valid_mask[:, :, None] * blocks, axis=1) / counts_float[:, None]
    centered = (
        (factor[:, :, None] * (blocks - column_mean[:, None, :]))
        .reshape(row_count, col_width)
        .astype(jnp.bfloat16)
    )
    series = observed.reshape(arc_total, arc_len)
    series_mean = jnp.sum(valid_mask * series, axis=1) / counts_float
    weighted = (factor * (series - series_mean[:, None])).reshape(row_count)
    arc_devices = lax.axis_size("arcs")
    tcol_devices = lax.axis_size("tcol")
    obs_total = row_count * arc_devices * tcol_devices
    rhs_part = jnp.dot(weighted, centered.astype(jnp.float32), precision=lax.Precision.HIGHEST)
    rhs = over_copies(rhs_part, ("arcs", "tcol")) * obs_total ** (-0.5)
    every_coef = lax.all_gather(centered, "trow", axis=1, tiled=True)
    full_width = every_coef.shape[1]
    narrow = full_width // (arc_devices * tcol_devices)
    shaped = every_coef.reshape(row_count, arc_devices, tcol_devices, narrow)
    moved = lax.all_to_all(shaped, "tcol", split_axis=2, concat_axis=0, tiled=True)
    right = moved.reshape(row_count * tcol_devices, arc_devices * narrow)
    partial_value = fold_with(right, lax.all_gather(centered, "tcol", axis=0, tiled=True))
    tile = sum_at_owner(partial_value.astype(jnp.bfloat16), "arcs", 1)
    gram = tile * (1.0 / obs_total)
    return (gram, rhs)


def solution(mesh):
    return jax.shard_map(
        local,
        mesh=mesh,
        in_specs=(
            P(("arcs", "tcol"), "trow"),
            P(("arcs", "tcol")),
            P(("arcs", "tcol")),
            P(("arcs", "tcol")),
        ),
        out_specs=(P("trow", ("arcs", "tcol")), P("trow")),
        check_vma=False,
    )
```

profile of v0, /device:TPU:1, one launch (start us, length us, event | category | flops | bytes accessed | tf_op | source)
XLA Modules:
  0.0 264.2 jit_solution(5195800618479505239)
XLA Ops:
  7.2 0.7 fusion.4
  7.9 0.7 convert_element_type.33
  8.6 0.7 reshape.101
  9.3 0.7 sqrt.3
  10.0 1.4 select_reduce_fusion
  11.4 1.2 multiply_reduce_fusion
  12.7 1.9 fusion.3
  14.6 0.7 all-gather.3.cloned.1.call-update
  15.3 33.9 %all-gather.5.cloned.1.call-done = bf16[128,12288]{1,0:T(8,128)(2,1)} async-done(((bf16[128,1536]{1,0:T(8,128)(2,1)}), bf16[128,12288]{1,0:T(8,128)(2,1)}) %all-gather.5.cloned.1.call-update) | async-done | bytes 3145744 | tf_op jit(solution)/shard_map/all_gather | solution.py:57
  49.2 3.5 %copy.21 = bf16[128,12288]{0,1:T(8,128)(2,1)S(1)} copy(bf16[128,12288]{1,0:T(8,128)(2,1)} %all-gather.5.cloned.1.call-done) | data formatting | bytes 6291456 | tf_op jit(solution)/shard_map/all_gather | solution.py:57
  52.7 1.9 copy.22
  54.6 9.4 %all-to-all-start = ((bf16[128,2,16,384]{0,3,1,2:T(8,128)(2,1)}), bf16[128,2,16,384]{0,3,1,2:T(8,128)(2,1)S(1)}, u32[]{:S(2)}, u32[]{:S(2)}) async-start(bf16[128,2,16,384]{0,3,1,2:T(8,128)(2,1)} %copy.22), calls=%async_computation | async-start | bytes 6291456 | tf_op jit(solution)/shard_map/all_to_all | solution.py:61
  64.0 0.7 convert_divide_fusion
  65.3 0.9 convolution_reduce_fusion
  66.3 82.1 %all-to-all-done = bf16[128,2,16,384]{0,3,1,2:T(8,128)(2,1)S(1)} async-done(((bf16[128,2,16,384]{0,3,1,2:T(8,128)(2,1)}), bf16[128,2,16,384]{0,3,1,2:T(8,128)(2,1)S(1)}, u32[]{:S(2)}, u32[]{:S(2)}) %all-to-all-start) | async-done | bytes 3145760 | tf_op jit(solution)/shard_map/all_to_all | solution.py:61
  148.4 0.8 broadcast_in_dim.2
  149.2 10.1 %all-to-all-start.2 = ((f32[32,1,1536]{2,1,0:T(1,128)}), f32[32,1,1536]{2,1,0:T(1,128)S(1)}, u32[]{:S(2)}, u32[]{:S(2)}) async-start(f32[32,1,1536]{2,1,0:T(1,128)} %broadcast_in_dim.2), calls=%async_computation.2 | async-start | bytes 393216 | tf_op jit(solution)/shard_map/all_to_all | solution.py:9
  159.2 3.7 %copy.23 = bf16[16,128,2,1,384]{1,0,4,2,3:T(8,128)(2,1)} copy(bf16[16,128,2,1,384]{1,4,2,0,3:T(8,128)(2,1)S(1)} %bitcast.27) | data formatting | bytes 6291456 | tf_op jit(solution)/shard_map/all_to_all | solution.py:61
  163.0 51.0 %all-gather.3.cloned.1.call-done = bf16[2048,1536]{1,0:T(8,128)(2,1)} async-done(((bf16[128,1536]{1,0:T(8,128)(2,1)}), bf16[2048,1536]{1,0:T(8,128)(2,1)}) %all-gather.3.cloned.1.call-update) | async-done | bytes 6291472 | tf_op jit(solution)/shard_map/all_gather | solution.py:63
  213.9 9.5 %convolution_convert_fusion = bf16[1536,768]{0,1:T(8,128)(2,1)} fusion(bf16[2048,1536]{1,0:T(8,128)(2,1)} %all-gather.3.cloned.1.call-done, bf16[96,8,16,128]{3,2,1,0:T(8,128)(2,1)} %bitcast.29), kind=kOutput, calls=%fused_computation.1 | convolution fusion | flops 4833017856 | bytes 11796480 | tf_op jit(solution)/shard_map/dot_general | solution.py:29
  223.4 3.8 %all-to-all-start.1 = ((bf16[2,1536,384]{1,2,0:T(8,128)(2,1)}), bf16[2,1536,384]{1,2,0:T(8,128)(2,1)S(1)}, u32[]{:S(2)}, u32[]{:S(2)}) async-start(bf16[2,1536,384]{1,2,0:T(8,128)(2,1)} %bitcast.30), calls=%async_computation.1 | async-start | bytes 4718592 | tf_op jit(solution)/shard_map/all_to_all | solution.py:24
  227.4 0.6 broadcast_multiply_fusion.1
  228.0 26.8 %all-to-all-done.1 = bf16[2,1536,384]{1,2,0:T(8,128)(2,1)S(1)} async-done(((bf16[2,1536,384]{1,2,0:T(8,128)(2,1)}), bf16[2,1536,384]{1,2,0:T(8,128)(2,1)S(1)}, u32[]{:S(2)}, u32[]{:S(2)}) %all-to-all-start.1) | async-done | bytes 2359328 | tf_op jit(solution)/shard_map/all_to_all | solution.py:24
  255.4 2.0 copy.25
  (17 shorter events, 1.7 us)
Async XLA Ops:
  7.2 42.0 %all-gather.5.cloned.1.call-start = ((), (), s32[]{:S(2)}) async-start(), calls=%async_computation.4 | async-start | bytes 3538944 | tf_op jit(solution)/shard_map/all_gather | solution.py:57
  14.6 199.3 %all-gather.3.cloned.1.call-start = ((), (), s32[]{:S(2)}) async-start(), calls=%async_computation.3 | async-start | bytes 6684672 | tf_op jit(solution)/shard_map/all_gather | solution.py:63
  54.6 9.4 %copy-start.2 = (s32[4]{0:T(128)S(1)}, s32[4]{0:T(128)}, u32[]{:S(2)}) copy-start(s32[4]{0:T(128)} %param.6) | copy-start | bytes 52
  54.6 10.7 %copy-start = (bf16[128,1536]{1,0:T(8,128)(2,1)S(1)}, bf16[128,1536]{1,0:T(8,128)(2,1)}, u32[]{:S(2)}) copy-start(bf16[128,1536]{1,0:T(8,128)(2,1)} %fusion.3) | copy-start | bytes 1179652
  54.6 10.7 %copy-start.1 = (f32[128]{0:T(128)S(1)}, f32[128]{0:T(128)}, u32[]{:S(2)}) copy-start(f32[128]{0:T(128)} %param.5) | copy-start | bytes 1540
  54.6 93.8 %all-to-all-start = ((bf16[128,2,16,384]{0,3,1,2:T(8,128)(2,1)}), bf16[128,2,16,384]{0,3,1,2:T(8,128)(2,1)S(1)}, u32[]{:S(2)}, u32[]{:S(2)}) async-start(bf16[128,2,16,384]{0,3,1,2:T(8,128)(2,1)} %copy.22), calls=%async_computation | async-start | bytes 6291456 | tf_op jit(solution)/shard_map/all_to_all | solution.py:61
  149.2 74.3 %all-to-all-start.2 = ((f32[32,1,1536]{2,1,0:T(1,128)}), f32[32,1,1536]{2,1,0:T(1,128)S(1)}, u32[]{:S(2)}, u32[]{:S(2)}) async-start(f32[32,1,1536]{2,1,0:T(1,128)} %broadcast_in_dim.2), calls=%async_computation.2 | async-start | bytes 393216 | tf_op jit(solution)/shard_map/all_to_all | solution.py:9
  223.4 31.3 %all-to-all-start.1 = ((bf16[2,1536,384]{1,2,0:T(8,128)(2,1)}), bf16[2,1536,384]{1,2,0:T(8,128)(2,1)S(1)}, u32[]{:S(2)}, u32[]{:S(2)}) async-start(bf16[2,1536,384]{1,2,0:T(8,128)(2,1)} %bitcast.30), calls=%async_computation.1 | async-start | bytes 4718592 | tf_op jit(solution)/shard_map/all_to_all | solution.py:24
Sparse Core Ops, SparseCore 0:
  14.7 34.4 all-gather.4
  52.2 161.6 all-gather.2
where the time goes:
time: 265 us; the launch traced here: 264 us
  waiting for transfers between devices  194 us (73%)
  starting transfers between devices  23.3 us (9%)
  between operations  14.1 us (5%)
  local copies, waits for them, and re-layouts  14 us (5%)
  matrix products  10.4 us (4%)
  other arithmetic  7.85 us (3%)
    all_to_all x1, waiting for transfers between devices, local(): lax.all_to_all(shaped, 'tcol', split_axis=2, concat_axis=0, tiled=True)  82.1 us
    all_gather x1, waiting for transfers between devices, local(): lax.all_gather(centered, 'tcol', axis=0, tiled=True)  51 us
    all_gather x1, waiting for transfers between devices, local(): every_coef = lax.all_gather(centered, 'trow', axis=1, tiled=True)  33.9 us
    all_to_all x1, waiting for transfers between devices, sum_at_owner(): lax.all_to_all(blocks, axis, split_axis=0, concat_axis=0, tiled=True)  26.8 us
    all_to_all x1, starting transfers between devices, from_everyone(): lax.all_to_all(jnp.broadcast_to(x[None], (devices, *x.shape)), axis, 0, 0...  10.1 us
    dot_general x1, matrix products, fold_with(): lax.dot_general(piece, right, (((0,), (0,)), ((), ())), preferred_element...  9.51 us
    all_to_all x1, starting transfers between devices, local(): lax.all_to_all(shaped, 'tcol', split_axis=2, concat_axis=0, tiled=True)  9.38 us
  transfers between devices with their start and end apart: 5, of which 4 were waited for; matrix products, arithmetic and copies ran while one was open for 8% of the time, Pallas kernels for 0%

commit v1 on v0

--- a/solution.py
+++ b/solution.py
@@ -2,6 +2,13 @@
 import jax.numpy as jnp
 from jax import lax
 from jax.sharding import PartitionSpec as P
+
+
+def manage_ticks_over_axis(arr_in, d_out):
+    later = list(arr_in.shape[1:])
+    later[d_out] *= arr_in.shape[0]
+    odd = jnp.moveaxis(arr_in, 0, d_out).reshape(later)
+    return odd
 
 
 def from_everyone(x, axis):
@@ -54,7 +61,26 @@
     obs_total = row_count * arc_devices * tcol_devices
     rhs_part = jnp.dot(weighted, centered.astype(jnp.float32), precision=lax.Precision.HIGHEST)
     rhs = over_copies(rhs_part, ("arcs", "tcol")) * obs_total ** (-0.5)
-    every_coef = lax.all_gather(centered, "trow", axis=1, tiled=True)
+    n_slots = lax.axis_size("trow")
+    lanes = []
+    for num in range(n_slots):
+        lanes.append((num, (num + 1) % n_slots))
+    items = []
+    for dd, src_i in lanes:
+        items.append((src_i, dd))
+    current_block, b_next = ([], [])
+    for p in range(n_slots - 1):
+        if p % 2 == 0:
+            current_block.append(
+                lax.ppermute(current_block[-1] if current_block else centered, "trow", lanes)
+            )
+        else:
+            b_next.append(lax.ppermute(b_next[-1] if b_next else centered, "trow", items))
+    left_arr = jnp.stack([*current_block[::-1], centered, *b_next], 0)
+    aux = lax.axis_index("trow")
+    w2 = aux - len(current_block)
+    left_arr = left_arr[(jnp.arange(n_slots) - w2) % n_slots]
+    every_coef = manage_ticks_over_axis(left_arr, 1)
     full_width = every_coef.shape[1]
     narrow = full_width // (arc_devices * tcol_devices)
     shaped = every_coef.reshape(row_count, arc_devices, tcol_devices, narrow)

time: 265 us -> 245 us (0.925)
  the two profiles are of different devices: /device:TPU:1 before, /device:TPU:24 now
where the time goes in v1:
time: 245 us
  waiting for transfers between devices  163 us (67%)
  starting transfers between devices  24.9 us (10%)
  local copies, waits for them, and re-layouts  24.2 us (10%)
  between operations  14.1 us (6%)
  matrix products  10.4 us (4%)
  other arithmetic  7.86 us (3%)
    all_to_all x1, waiting for transfers between devices, local(): lax.all_to_all(shaped, 'tcol', split_axis=2, concat_axis=0, tiled=True)  113 us
    all_to_all x1, waiting for transfers between devices, sum_at_owner(): lax.all_to_all(blocks, axis, split_axis=0, concat_axis=0, tiled=True)  27.4 us
    ppermute x4, waiting for transfers between devices, local(): lax.ppermute(current_block[-1] if current_block else centered, 'trow', la...  22.9 us
    all_to_all x1, starting transfers between devices, local(): lax.all_to_all(shaped, 'tcol', split_axis=2, concat_axis=0, tiled=True)  11.2 us
    dot_general x1, matrix products, fold_with(): lax.dot_general(piece, right, (((0,), (0,)), ((), ())), preferred_element...  9.51 us
    unnamed x14, local copies, waits for them, and re-layouts  7.42 us
  transfers between devices with their start and end apart: 11, of which 6 were waited for; matrix products, arithmetic and copies ran while one was open for 13% of the time, Pallas kernels for 0%

profile of v1, /device:TPU:24, one launch (start us, length us, event | category | flops | bytes accessed | tf_op | source)
XLA Modules:
  0.0 244.9 jit_solution(1781045762818310576)
XLA Ops:
  10.0 1.4 select_reduce_fusion
  11.4 1.2 multiply_reduce_fusion
  12.7 1.9 fusion.3
  14.6 7.4 %collective-permute-done = bf16[128,1536]{1,0:T(8,128)(2,1)S(1)} collective-permute-done((bf16[128,1536]{1,0:T(8,128)(2,1)}, bf16[128,1536]{1,0:T(8,128)(2,1)S(1)}, u32[]{:S(2)}, u32[]{:S(2)}) %collective-permute-start) | collective-permute-done | bytes 393248 | tf_op jit(solution)/shard_map/ppermute | solution.py:75
  22.0 1.7 collective-permute-start.4
  23.8 5.5 %collective-permute-done.1 = bf16[128,1536]{1,0:T(8,128)(2,1)S(1)} collective-permute-done((bf16[128,1536]{1,0:T(8,128)(2,1)S(1)}, bf16[128,1536]{1,0:T(8,128)(2,1)S(1)}, u32[]{:S(2)}, u32[]{:S(2)}) %collective-permute-start.1) | collective-permute-done | bytes 393248 | tf_op jit(solution)/shard_map/ppermute | solution.py:75
  30.0 1.2 collective-permute-start.5
  31.2 5.2 %collective-permute-done.2 = bf16[128,1536]{1,0:T(8,128)(2,1)S(1)} collective-permute-done((bf16[128,1536]{1,0:T(8,128)(2,1)S(1)}, bf16[128,1536]{1,0:T(8,128)(2,1)S(1)}, u32[]{:S(2)}, u32[]{:S(2)}) %collective-permute-start.2) | collective-permute-done | bytes 393248 | tf_op jit(solution)/shard_map/ppermute | solution.py:75
  36.4 2.0 collective-permute-start.3
  38.8 4.8 %collective-permute-done.3 = bf16[128,1536]{1,0:T(8,128)(2,1)S(1)} collective-permute-done((bf16[128,1536]{1,0:T(8,128)(2,1)S(1)}, bf16[128,1536]{1,0:T(8,128)(2,1)S(1)}, u32[]{:S(2)}, u32[]{:S(2)}) %collective-permute-start.3) | collective-permute-done | bytes 393248 | tf_op jit(solution)/shard_map/ppermute | solution.py:75
  47.5 0.8 bitcast_dynamic-update-slice_fusion.2
  48.3 0.8 bitcast_dynamic-update-slice_fusion.1
  49.9 2.6 %gather_fusion = bf16[8,128,1536]{2,1,0:T(8,128)(2,1)S(1)} fusion(bf16[8,128,1536]{2,1,0:T(8,128)(2,1)} %bitcast_dynamic-update-slice_fusion, s32[1024]{0:T(1024)S(1)} %pad_clamp_fusion), kind=kCustom, calls=%fused_computation | custom fusion | bytes 6291488 | tf_op jit(solution)/shard_map/gather | solution.py:82
  52.5 2.8 %copy.17 = bf16[128,8,1536]{0,2,1:T(8,128)(2,1)} copy(bf16[128,8,1536]{2,0,1:T(8,128)(2,1)S(1)} %bitcast.47) | data formatting | bytes 6291456 | tf_op jit(solution)/shard_map/transpose | solution.py:10
  55.4 3.9 %copy.18 = bf16[128,2,16,384]{0,3,1,2:T(8,128)(2,1)} copy(bf16[128,2,16,384]{0,3,2,1:T(8,128)(2,1)} %bitcast.48) | data formatting | bytes 6291456 | tf_op jit(solution)/shard_map/reshape;reshape | solution.py:86
  59.2 11.2 %all-to-all-start = ((bf16[128,2,16,384]{0,3,1,2:T(8,128)(2,1)}), bf16[128,2,16,384]{0,3,1,2:T(8,128)(2,1)S(1)}, u32[]{:S(2)}, u32[]{:S(2)}) async-start(bf16[128,2,16,384]{0,3,1,2:T(8,128)(2,1)} %copy.18), calls=%async_computation | async-start | bytes 6291456 | tf_op jit(solution)/shard_map/all_to_all | solution.py:87
  71.8 0.9 convolution_reduce_fusion
  72.7 112.9 %all-to-all-done = bf16[128,2,16,384]{0,3,1,2:T(8,128)(2,1)S(1)} async-done(((bf16[128,2,16,384]{0,3,1,2:T(8,128)(2,1)}), bf16[128,2,16,384]{0,3,1,2:T(8,128)(2,1)S(1)}, u32[]{:S(2)}, u32[]{:S(2)}) %all-to-all-start) | async-done | bytes 3145760 | tf_op jit(solution)/shard_map/all_to_all | solution.py:87
  186.4 3.9 %all-to-all-start.2 = ((f32[32,1,1536]{2,1,0:T(1,128)}), f32[32,1,1536]{2,1,0:T(1,128)S(1)}, u32[]{:S(2)}, u32[]{:S(2)}) async-start(f32[32,1,1536]{2,1,0:T(1,128)} %broadcast_in_dim.2), calls=%async_computation.2 | async-start | bytes 393216 | tf_op jit(solution)/shard_map/all_to_all | solution.py:16
  190.2 3.7 %copy.19 = bf16[16,128,2,1,384]{1,0,4,2,3:T(8,128)(2,1)} copy(bf16[16,128,2,1,384]{1,4,2,0,3:T(8,128)(2,1)S(1)} %bitcast.46) | data formatting | bytes 6291456 | tf_op jit(solution)/shard_map/all_to_all | solution.py:87
  194.0 9.5 %convolution_convert_fusion = bf16[1536,768]{0,1:T(8,128)(2,1)} fusion(bf16[2048,1536]{1,0:T(8,128)(2,1)} %all-gather.2.cloned.1.call-done, bf16[96,8,16,128]{3,2,1,0:T(8,128)(2,1)} %bitcast.49), kind=kOutput, calls=%fused_computation.2 | convolution fusion | flops 4833017856 | bytes 11796480 | tf_op jit(solution)/shard_map/dot_general | solution.py:36
  203.5 3.8 %all-to-all-start.1 = ((bf16[2,1536,384]{1,2,0:T(8,128)(2,1)}), bf16[2,1536,384]{1,2,0:T(8,128)(2,1)S(1)}, u32[]{:S(2)}, u32[]{:S(2)}) async-start(bf16[2,1536,384]{1,2,0:T(8,128)(2,1)} %bitcast.50), calls=%async_computation.1 | async-start | bytes 4718592 | tf_op jit(solution)/shard_map/all_to_all | solution.py:31
  208.0 27.4 %all-to-all-done.1 = bf16[2,1536,384]{1,2,0:T(8,128)(2,1)S(1)} async-done(((bf16[2,1536,384]{1,2,0:T(8,128)(2,1)}), bf16[2,1536,384]{1,2,0:T(8,128)(2,1)S(1)}, u32[]{:S(2)}, u32[]{:S(2)}) %all-to-all-start.1) | async-done | bytes 2359328 | tf_op jit(solution)/shard_map/all_to_all | solution.py:31
  236.1 2.0 copy.21
  (39 shorter events, 12.2 us)
Async XLA Ops:
  7.2 186.8 %all-gather.2.cloned.1.call-start = ((), (), s32[]{:S(2)}) async-start(), calls=%async_computation.3 | async-start | bytes 6684672 | tf_op jit(solution)/shard_map/all_gather | solution.py:89
  14.6 32.1 %copy-start = (bf16[128,1536]{1,0:T(8,128)(2,1)S(1)}, bf16[128,1536]{1,0:T(8,128)(2,1)}, u32[]{:S(2)}) copy-start(bf16[128,1536]{1,0:T(8,128)(2,1)} %fusion.3) | copy-start | bytes 1179652
  14.6 7.4 %collective-permute-start = (bf16[128,1536]{1,0:T(8,128)(2,1)}, bf16[128,1536]{1,0:T(8,128)(2,1)S(1)}, u32[]{:S(2)}, u32[]{:S(2)}) collective-permute-start(bf16[128,1536]{1,0:T(8,128)(2,1)} %fusion.3), channel_id=1, source_target_pairs={{0,16},{16,32},{32,48},{48,64},{64,80},{80,96},{96,112},{112,0},{1... | collective-permute-start | bytes 1179656 | tf_op jit(solution)/shard_map/ppermute | solution.py:75
  22.0 7.2 %collective-permute-start.1 = (bf16[128,1536]{1,0:T(8,128)(2,1)S(1)}, bf16[128,1536]{1,0:T(8,128)(2,1)S(1)}, u32[]{:S(2)}, u32[]{:S(2)}) collective-permute-start(bf16[128,1536]{1,0:T(8,128)(2,1)S(1)} %collective-permute-done), channel_id=1, source_target_pairs={{0,16},{16,32},{32,48},{48,64},{64,80},{80,96},{96,112},{112,0},{1... | collective-permute-start | bytes 1179656 | tf_op jit(solution)/shard_map/ppermute | solution.py:75
  22.0 8.0 %collective-permute-start.4 = (bf16[128,1536]{1,0:T(8,128)(2,1)}, bf16[128,1536]{1,0:T(8,128)(2,1)S(1)}, u32[]{:S(2)}, u32[]{:S(2)}) collective-permute-start(bf16[128,1536]{1,0:T(8,128)(2,1)} %fusion.3), channel_id=1, source_target_pairs={{16,0},{32,16},{48,32},{64,48},{80,64},{96,80},{112,96},{0,112},{1... | collective-permute-start | bytes 1179656 | tf_op jit(solution)/shard_map/ppermute | solution.py:78
  29.2 7.2 %collective-permute-start.2 = (bf16[128,1536]{1,0:T(8,128)(2,1)S(1)}, bf16[128,1536]{1,0:T(8,128)(2,1)S(1)}, u32[]{:S(2)}, u32[]{:S(2)}) collective-permute-start(bf16[128,1536]{1,0:T(8,128)(2,1)S(1)} %collective-permute-done.1), channel_id=1, source_target_pairs={{0,16},{16,32},{32,48},{48,64},{64,80},{80,96},{96,112},{112,0},{1... | collective-permute-start | bytes 1179656 | tf_op jit(solution)/shard_map/ppermute | solution.py:75
  30.0 8.4 %collective-permute-start.5 = (bf16[128,1536]{1,0:T(8,128)(2,1)S(1)}, bf16[128,1536]{1,0:T(8,128)(2,1)S(1)}, u32[]{:S(2)}, u32[]{:S(2)}) collective-permute-start(bf16[128,1536]{1,0:T(8,128)(2,1)S(1)} %collective-permute-done.4), channel_id=1, source_target_pairs={{16,0},{32,16},{48,32},{64,48},{80,64},{96,80},{112,96},{0,112},{1... | collective-permute-start | bytes 1179656 | tf_op jit(solution)/shard_map/ppermute | solution.py:78
  36.4 7.2 %collective-permute-start.3 = (bf16[128,1536]{1,0:T(8,128)(2,1)S(1)}, bf16[128,1536]{1,0:T(8,128)(2,1)S(1)}, u32[]{:S(2)}, u32[]{:S(2)}) collective-permute-start(bf16[128,1536]{1,0:T(8,128)(2,1)S(1)} %collective-permute-done.2), channel_id=1, source_target_pairs={{0,16},{16,32},{32,48},{48,64},{64,80},{80,96},{96,112},{112,0},{1... | collective-permute-start | bytes 1179656 | tf_op jit(solution)/shard_map/ppermute | solution.py:75
  38.4 10.6 %collective-permute-start.6 = (bf16[128,1536]{1,0:T(8,128)(2,1)S(1)}, bf16[128,1536]{1,0:T(8,128)(2,1)S(1)}, u32[]{:S(2)}, u32[]{:S(2)}) collective-permute-start(bf16[128,1536]{1,0:T(8,128)(2,1)S(1)} %collective-permute-done.5), channel_id=1, source_target_pairs={{16,0},{32,16},{48,32},{64,48},{80,64},{96,80},{112,96},{0,112},{1... | collective-permute-start | bytes 1179656 | tf_op jit(solution)/shard_map/ppermute | solution.py:78
  59.2 11.2 %copy-start.2 = (s32[4]{0:T(128)S(1)}, s32[4]{0:T(128)}, u32[]{:S(2)}) copy-start(s32[4]{0:T(128)} %param.6) | copy-start | bytes 52
  59.2 12.5 %copy-start.1 = (f32[128]{0:T(128)S(1)}, f32[128]{0:T(128)}, u32[]{:S(2)}) copy-start(f32[128]{0:T(128)} %param.5) | copy-start | bytes 1540
  59.2 126.3 %all-to-all-start = ((bf16[128,2,16,384]{0,3,1,2:T(8,128)(2,1)}), bf16[128,2,16,384]{0,3,1,2:T(8,128)(2,1)S(1)}, u32[]{:S(2)}, u32[]{:S(2)}) async-start(bf16[128,2,16,384]{0,3,1,2:T(8,128)(2,1)} %copy.18), calls=%async_computation | async-start | bytes 6291456 | tf_op jit(solution)/shard_map/all_to_all | solution.py:87
  186.4 17.1 %all-to-all-start.2 = ((f32[32,1,1536]{2,1,0:T(1,128)}), f32[32,1,1536]{2,1,0:T(1,128)S(1)}, u32[]{:S(2)}, u32[]{:S(2)}) async-start(f32[32,1,1536]{2,1,0:T(1,128)} %broadcast_in_dim.2), calls=%async_computation.2 | async-start | bytes 393216 | tf_op jit(solution)/shard_map/all_to_all | solution.py:16
  203.5 32.0 %all-to-all-start.1 = ((bf16[2,1536,384]{1,2,0:T(8,128)(2,1)}), bf16[2,1536,384]{1,2,0:T(8,128)(2,1)S(1)}, u32[]{:S(2)}, u32[]{:S(2)}) async-start(bf16[2,1536,384]{1,2,0:T(8,128)(2,1)} %bitcast.50), calls=%async_computation.1 | async-start | bytes 4718592 | tf_op jit(solution)/shard_map/all_to_all | solution.py:31
Sparse Core Ops, SparseCore 0:
  14.7 154.6 all-gather.1
